TPU v7x, 32 devices: a whole 2x2x4 slice. The times are simulated.
32 devices in a mesh: ta: 4 (over y, x), sa: 8 (over z, core).
Axes of the slice: x: 2, y: 2, z: 4, core: 2. Of those that a mesh axis runs over, the one named last changes fastest.
Arguments:
- eigvecs: float32 [2, 8, 64, 3, 4096], P(None, 'ta', None, None, 'sa'), may hold values from -0.0546875 to 0.0546875
- solutions: float32 [2, 8, 3, 8, 4, 3, 4096], P(None, 'ta', None, None, None, None, 'sa'), may hold values from -15 to 15
- source_times: int32 [3], replicated, may hold values from 0 to 7, as said below
- spin_dilution: int32 [3, 8], replicated, may hold values from 0 to 3
Outputs:
- perambulator: float32 [2, 8, 6144], P(None, 'ta', 'sa')
- norms: float32 [3, 8], replicated
Inputs may be any that keep to these rules, and one draw needn't show every extreme that they name: `source_times`: some source lies at slice 0 and another at slice 8 - 1.
All inputs are finite; a program needn't handle non-finite values.
Results may differ from a plain program's by a relative error of at most 0.000084.
Values sent between devices are 32-bit elements; how exact they have to be, the bound alone decides.
No kernel may reach another device: no remote copies, remote signals or barrier semaphores. Data moves between devices by JAX's collectives and lax.ppermute only.
A program may use at most 64 MiB of HBM per device.

v0:
```python
import jax
import jax.numpy as jnp
from jax import lax
from jax.sharding import PartitionSpec as P


def on_device(eigvecs, solutions, source_times, spin_dilution):
    time_rows = eigvecs.shape[1]
    eig_count = eigvecs.shape[2]
    site_count = eigvecs.shape[4]
    src_count = spin_dilution.shape[0]
    col_count = spin_dilution.shape[1]
    columns = src_count * col_count * 4
    inner_len = 3 * site_count
    all_cells = 12.0 * time_rows * lax.axis_size("ta") * site_count * lax.axis_size("sa")
    norm_parts = jnp.sum(solutions * solutions, axis=(0, 1, 4, 5, 6))
    eigen_rows = eigvecs.reshape(2, time_rows, eig_count, inner_len)
    solution_rows = solutions.reshape(2, time_rows, columns, inner_len)
    precise = lax.Precision.HIGHEST
    upper_half = jnp.concatenate([eigen_rows[0], eigen_rows[1]], axis=2)
    lower_half = jnp.concatenate([-eigen_rows[1], eigen_rows[0]], axis=2)
    left_side = jnp.concatenate([upper_half, lower_half], axis=1)
    right_side = jnp.concatenate([solution_rows[0], solution_rows[1]], axis=2)
    stacked = jnp.einsum(
        "tmk,tnk->tmn", left_side, right_side, precision=precise, preferred_element_type=jnp.float32
    )
    real_part = stacked[:, :eig_count]
    imag_part = stacked[:, eig_count:]
    slice_times = lax.axis_index("ta") * time_rows + jnp.arange(time_rows, dtype=jnp.int32)
    boundary = jnp.where(slice_times[:, None] < source_times[None, :], -1.0, 1.0).astype(
        jnp.float32
    )
    chirality = jnp.where(spin_dilution < 2, 1.0, -1.0).astype(jnp.float32)
    signs = jnp.broadcast_to(
        (boundary[:, :, None] * chirality[None])[:, :, :, None],
        (time_rows, src_count, col_count, 4),
    ).reshape(time_rows, columns)
    partial_value = (jnp.stack([real_part, imag_part]) * signs[None, :, None, :]).reshape(
        2, time_rows, eig_count * columns
    )
    own_width = eig_count * columns // lax.axis_size("sa")
    own_start = lax.axis_index("sa") * own_width
    norm_total = lax.psum(norm_parts, ("ta", "sa"))
    summed = lax.psum(partial_value, "sa")
    perambulator = lax.dynamic_slice_in_dim(summed, own_start, own_width, 2)
    return (perambulator, norm_total / all_cells)


def solution(mesh):
    return jax.shard_map(
        on_device,
        mesh=mesh,
        in_specs=(
            P(None, "ta", None, None, "sa"),
            P(None, "ta", None, None, None, None, "sa"),
            P(),
            P(),
        ),
        out_specs=(P(None, "ta", "sa"), P()),
        check_vma=False,
    )
```

profile of v0, /device:TPU:8, one launch (start us, length us, event | category | flops | bytes accessed | tf_op | source)
XLA Modules:
  0.0 92.8 jit_solution(17779468733230858066)
XLA Ops:
  7.2 0.0 all-reduce.2.cloned.1.call-start
  7.2 0.0 copy-start
  7.2 3.3 %fusion.12 = (f32[1,2,3,8,4,3,512]{6,4,5,3,2,1,0:T(4,128)S(1)}, f32[1,2,3,8,4,3,512]{6,4,5,3,2,1,0:T(4,128)}) fusion(f32[2,2,3,8,4,3,512]{6,4,5,3,2,1,0:T(4,128)} %param.5), kind=kLoop, calls=%fused_computation.20 | loop fusion | bytes 4718592 | tf_op jit(solution)/shard_map/slice | solution.py:23
  10.6 0.0 copy-done
  10.6 0.0 copy-start.1
  10.6 0.6 multiply_reduce_fusion
  11.1 0.8 copy-done.1
  12.0 0.1 fusion.13
  12.1 0.5 copy.10
  12.6 1.5 %squeeze.14 = f32[2,64,1536]{2,1,0:T(8,128)} reshape(f32[1,2,64,3,512]{4,3,2,1,0:T(4,128)S(1)} %copy.10) | data formatting | bytes 1572864 | tf_op jit(solution)/shard_map/squeeze | solution.py:20
  14.1 0.5 copy.11
  14.7 0.6 squeeze.15
  15.3 0.9 %neg.3 = f32[2,64,1536]{2,1,0:T(8,128)} negate(f32[2,64,1536]{2,1,0:T(8,128)S(1)} %squeeze.15) | non-fusion elementwise | flops 196608 | bytes 1572864 | tf_op jit(solution)/shard_map/neg | solution.py:21
  16.2 1.9 %copy.13 = f32[1,2,3,8,4,3,512]{6,5,4,3,2,1,0:T(4,128)S(1)} copy(f32[1,2,3,8,4,3,512]{6,4,5,3,2,1,0:T(4,128)} %get-tuple-element.3) | data formatting | bytes 2359296 | tf_op jit(solution)/shard_map/slice | solution.py:23
  18.1 1.7 %squeeze.17 = f32[2,96,1536]{2,1,0:T(8,128)} reshape(f32[1,2,3,8,4,3,512]{6,5,4,3,2,1,0:T(4,128)S(1)} %copy.13) | data formatting | bytes 2359296 | tf_op jit(solution)/shard_map/squeeze | solution.py:23
  19.9 0.7 copy.12
  20.5 0.0 copy-start.2
  20.6 1.7 %squeeze.16 = f32[2,96,1536]{2,1,0:T(8,128)} reshape(f32[1,2,3,8,4,3,512]{6,5,4,3,2,1,0:T(4,128)S(1)} %copy.12) | data formatting | bytes 2359296 | tf_op jit(solution)/shard_map/squeeze | solution.py:23
  22.3 0.0 copy-done.2
  22.3 0.0 copy-start.3
  22.3 0.0 copy-start.4
  22.3 5.4 %fusion = f32[2,128,96]{1,2,0:T(8,128)S(1)} fusion(f32[2,64,1536]{2,1,0:T(8,128)} %squeeze.14, f32[2,64,1536]{2,1,0:T(8,128)} %neg.3, f32[2,64,1536]{2,1,0:T(8,128)S(1)} %squeeze.15, f32[2,96,1536]{2,1,0:T(8,128)S(1)} %copy-done.2, f32[2,96,1536]{2,1,0:T(8,128)} %squeeze.16), kind=kOutput, calls=%fused_computation | convolution fusion | flops 908918784 | bytes 4816896 | tf_op jit(solution)/shard_map/tmk,tnk->tmn/dot_general | solution.py:24
  27.6 0.1 fusion.14
  27.7 0.1 copy.15
  27.8 0.1 stack.10
  28.0 0.1 copy.14
  28.0 0.1 stack.9
  28.2 0.0 copy-done.3
  28.2 0.0 copy-done.4
  28.2 0.1 compare_select_fusion.1
  28.3 0.1 broadcast_multiply_fusion
  28.4 0.1 broadcast_in_dim.30
  28.4 0.1 mul.45
  28.6 0.1 mul.47
  28.7 0.7 maximum_multiply_fusion
  29.4 0.0 all-reduce.2.cloned.1.call-update
  29.4 40.5 %psum.15 = f32[3,8]{1,0:T(4,128)S(1)} all-reduce(f32[3,8]{1,0:T(4,128)S(1)} %multiply_reduce_fusion), channel_id=1, replica_groups=mesh['ta'=4,'sa'=8] {'ta','sa'}, use_global_device_ids=true, to_apply=%region_2.3 | all-reduce | flops 24 | bytes 192 | tf_op jit(solution)/shard_map/psum | solution.py:43
  69.9 0.6 broadcast_multiply_fusion.1
  70.4 14.2 %all-reduce.2.cloned.1.call-done = f32[2,2,6144]{2,1,0:T(2,128)} async-done(((f32[2,2,6144]{2,1,0:T(2,128)}), f32[2,2,6144]{2,1,0:T(2,128)}) %all-reduce.2.cloned.1.call-update) | async-done | bytes 98320 | tf_op jit(solution)/shard_map/psum | solution.py:44
  84.7 1.3 %constant_dynamic-slice_fusion = f32[2,2,768]{2,1,0:T(2,128)} fusion(f32[2,2,6144]{2,1,0:T(2,128)} %all-reduce.2.cloned.1.call-done, s32[]{:T(128)S(6)} %select_n.17), kind=kLoop, calls=%fused_computation.18 | loop fusion | bytes 24580 | tf_op jit(solution)/shard_map/dynamic_slice | solution.py:45
  (3 shorter events, 0.0 us)
Async XLA Ops:
  7.2 77.5 %all-reduce.2.cloned.1.call-start = ((), (), s32[]{:S(2)}) async-start(), calls=%async_computation | async-start | bytes 196608 | tf_op jit(solution)/shard_map/psum | solution.py:44
  7.2 3.3 %copy-start = (f32[2,2,3,8,4,3,512]{6,4,5,3,2,1,0:T(4,128)S(1)}, f32[2,2,3,8,4,3,512]{6,4,5,3,2,1,0:T(4,128)}, u32[]{:S(2)}) copy-start(f32[2,2,3,8,4,3,512]{6,4,5,3,2,1,0:T(4,128)} %param.5) | copy-start | bytes 7077892
  10.6 1.4 %copy-start.1 = (f32[2,2,64,3,512]{4,2,3,1,0:T(8,128)S(1)}, f32[2,2,64,3,512]{4,2,3,1,0:T(8,128)}, u32[]{:S(2)}) copy-start(f32[2,2,64,3,512]{4,2,3,1,0:T(8,128)} %param.4) | copy-start | bytes 4718596
  20.5 1.7 %copy-start.2 = (f32[2,96,1536]{2,1,0:T(8,128)S(1)}, f32[2,96,1536]{2,1,0:T(8,128)}, u32[]{:S(2)}) copy-start(f32[2,96,1536]{2,1,0:T(8,128)} %squeeze.17) | copy-start | bytes 3538948
  22.3 5.9 %copy-start.3 = (s32[3,8]{1,0:T(4,128)S(1)}, s32[3,8]{1,0:T(4,128)}, u32[]{:S(2)}) copy-start(s32[3,8]{1,0:T(4,128)} %param.7) | copy-start | bytes 292
  22.3 5.9 %copy-start.4 = (s32[3]{0:T(128)S(1)}, s32[3]{0:T(128)}, u32[]{:S(2)}) copy-start(s32[3]{0:T(128)} %param.6) | copy-start | bytes 40
Sparse Core Ops, SparseCore 0:
  29.5 55.1 all-reduce.1
where the time goes:
time: 93.2 us; the launch traced here: 92.8 us
  blocking collectives  40.5 us (43%)
  local copies, waits for them, and re-layouts  15.6 us (17%)
  waiting for transfers between devices  14.3 us (15%)
  between operations  14.2 us (15%)
  matrix products  5.36 us (6%)
  other arithmetic  2.95 us (3%)
    psum x1, blocking collectives, on_device(): norm_total = lax.psum(norm_parts, ('ta', 'sa'))  40.5 us
    psum x1, waiting for transfers between devices, on_device(): summed = lax.psum(partial_value, 'sa')  14.2 us
    slice x3, local copies, waits for them, and re-layouts, on_device(): right_side = jnp.concatenate([solution_rows[0], solution_rows[1]], axis=2)  5.92 us
    dot_general x1, matrix products, on_device(): jnp.einsum('tmk,tnk->tmn', left_side, right_side, precision=precise, pref...  5.36 us
    squeeze x2, local copies, waits for them, and re-layouts, on_device(): right_side = jnp.concatenate([solution_rows[0], solution_rows[1]], axis=2)  3.46 us
    squeeze x2, local copies, waits for them, and re-layouts, on_device(): upper_half = jnp.concatenate([eigen_rows[0], eigen_rows[1]], axis=2)  2.07 us
  transfers between devices with their start and end apart: 1, of which 1 were waited for; matrix products, arithmetic and copies ran while one was open for 1% of the time, Pallas kernels for 0%

commit v1 on v0

--- a/solution.py
+++ b/solution.py
@@ -41,7 +41,8 @@
     own_width = eig_count * columns // lax.axis_size("sa")
     own_start = lax.axis_index("sa") * own_width
     norm_total = lax.psum(norm_parts, ("ta", "sa"))
-    summed = lax.psum(partial_value, "sa")
+    pieces = lax.all_gather(partial_value, "sa", axis=0, tiled=False)
+    summed = pieces.sum(axis=0)
     perambulator = lax.dynamic_slice_in_dim(summed, own_start, own_width, 2)
     return (perambulator, norm_total / all_cells)
 

time: 93.2 us -> 87 us (0.933); the launches traced: 92.8 us -> 85.3 us
  blocking collectives: 40.5 us -> 56.1 us
  waiting for transfers between devices: 14.3 us -> 0 us
  between operations: 14.2 us -> 0.75 us
  local copies, waits for them, and re-layouts: 15.6 us -> 19 us
    all_gather x0 -> x1, blocking collectives: none -> 15.8 us  [on_device(): pieces = lax.all_gather(partial_value, 'sa', axis=0, tiled=False)]
    psum x1 -> x0, waiting for transfers between devices: 14.2 us -> none  [on_device(): summed = lax.psum(partial_value, 'sa')]
    slice x3, local copies, waits for them, and re-layouts: 1.2 us -> 4.73 us  [on_device(): upper_half = jnp.concatenate([eigen_rows[0], eigen_rows[1]], axis=2)]
    squeeze x2, local copies, waits for them, and re-layouts: 3.46 us -> 5.76 us  [on_device(): right_side = jnp.concatenate([solution_rows[0], solution_rows[1]], axis=2)]
    slice x3, local copies, waits for them, and re-layouts: 5.92 us -> 4.1 us  [on_device(): right_side = jnp.concatenate([solution_rows[0], solution_rows[1]], axis=2)]
    neg x1, other arithmetic: 0.93 us -> 2.09 us  [on_device(): lower_half = jnp.concatenate([-eigen_rows[1], eigen_rows[0]], axis=2)]
  transfers between devices with their start and end apart: 1 -> 0, of which waited for: 1 -> 0; matrix products, arithmetic and copies ran while one was open for 1% -> 0% of each run, Pallas kernels for 0% -> 0%
where the time goes in v1:
time: 87 us; the launch traced here: 85.3 us
  blocking collectives  56.1 us (64%)
  local copies, waits for them, and re-layouts  19 us (22%)
  matrix products  5.72 us (7%)
  other arithmetic  3.79 us (4%)
    psum x1, blocking collectives, on_device(): norm_total = lax.psum(norm_parts, ('ta', 'sa'))  40.3 us
    all_gather x1, blocking collectives, on_device(): pieces = lax.all_gather(partial_value, 'sa', axis=0, tiled=False)  15.8 us
    squeeze x2, local copies, waits for them, and re-layouts, on_device(): right_side = jnp.concatenate([solution_rows[0], solution_rows[1]], axis=2)  5.76 us
    dot_general x1, matrix products, on_device(): jnp.einsum('tmk,tnk->tmn', left_side, right_side, precision=precise, pref...  5.72 us
    slice x3, local copies, waits for them, and re-layouts, on_device(): upper_half = jnp.concatenate([eigen_rows[0], eigen_rows[1]], axis=2)  4.73 us
    slice x3, local copies, waits for them, and re-layouts, on_device(): right_side = jnp.concatenate([solution_rows[0], solution_rows[1]], axis=2)  4.1 us
    squeeze x2, local copies, waits for them, and re-layouts, on_device(): upper_half = jnp.concatenate([eigen_rows[0], eigen_rows[1]], axis=2)  2.99 us
    neg x1, other arithmetic, on_device(): lower_half = jnp.concatenate([-eigen_rows[1], eigen_rows[0]], axis=2)  2.09 us

profile of v1, /device:TPU:8, one launch (start us, length us, event | category | flops | bytes accessed | tf_op | source)
XLA Modules:
  0.0 85.3 jit_solution(319339221131711183)
XLA Ops:
  0.6 2.4 %fusion.13 = (f32[1,2,64,3,512]{4,2,3,1,0:T(8,128)}, f32[1,2,64,3,512]{4,2,3,1,0:T(8,128)S(1)}) fusion(f32[2,2,64,3,512]{4,2,3,1,0:T(8,128)} %param.4), kind=kLoop, calls=%fused_computation.21 | loop fusion | bytes 3145728 | tf_op jit(solution)/shard_map/slice | solution.py:20
  3.0 0.5 copy.16
  3.5 1.5 %squeeze.14 = f32[2,64,1536]{2,1,0:T(8,128)} reshape(f32[1,2,64,3,512]{4,3,2,1,0:T(4,128)S(1)} %copy.16) | data formatting | bytes 1572864 | tf_op jit(solution)/shard_map/squeeze | solution.py:20
  5.0 0.0 copy-start
  5.0 1.8 %copy.17 = f32[1,2,64,3,512]{4,3,2,1,0:T(4,128)S(1)} copy(f32[1,2,64,3,512]{4,2,3,1,0:T(8,128)} %get-tuple-element.4) | data formatting | bytes 1572864 | tf_op jit(solution)/shard_map/slice | solution.py:20
  6.8 1.5 %squeeze.15 = f32[2,64,1536]{2,1,0:T(8,128)} reshape(f32[1,2,64,3,512]{4,3,2,1,0:T(4,128)S(1)} %copy.17) | data formatting | bytes 1572864 | tf_op jit(solution)/shard_map/squeeze | solution.py:20
  8.4 2.1 %neg.3 = f32[2,64,1536]{2,1,0:T(8,128)} negate(f32[2,64,1536]{2,1,0:T(8,128)} %squeeze.15) | non-fusion elementwise | flops 196608 | bytes 1572864 | tf_op jit(solution)/shard_map/neg | solution.py:21
  10.4 0.0 copy-done
  10.5 0.5 fusion.12
  10.9 1.8 %copy.19 = f32[1,2,3,8,4,3,512]{6,5,4,3,2,1,0:T(4,128)} copy(f32[1,2,3,8,4,3,512]{6,4,5,3,2,1,0:T(4,128)S(1)} %get-tuple-element.3) | data formatting | bytes 2359296 | tf_op jit(solution)/shard_map/slice | solution.py:23
  12.8 2.8 %squeeze.17 = f32[2,96,1536]{2,1,0:T(8,128)} reshape(f32[1,2,3,8,4,3,512]{6,5,4,3,2,1,0:T(4,128)} %copy.19) | data formatting | bytes 2359296 | tf_op jit(solution)/shard_map/squeeze | solution.py:23
  15.6 1.8 %copy.18 = f32[1,2,3,8,4,3,512]{6,5,4,3,2,1,0:T(4,128)} copy(f32[1,2,3,8,4,3,512]{6,4,5,3,2,1,0:T(4,128)S(1)} %get-tuple-element.2) | data formatting | bytes 2359296 | tf_op jit(solution)/shard_map/slice | solution.py:23
  17.4 0.0 copy-start.1
  17.4 2.9 %squeeze.16 = f32[2,96,1536]{2,1,0:T(8,128)} reshape(f32[1,2,3,8,4,3,512]{6,5,4,3,2,1,0:T(4,128)} %copy.18) | data formatting | bytes 2359296 | tf_op jit(solution)/shard_map/squeeze | solution.py:23
  20.3 0.0 copy-done.1
  20.3 0.0 copy-start.2
  20.3 0.0 copy-start.3
  20.3 5.7 %fusion = f32[2,128,96]{1,2,0:T(8,128)S(1)} fusion(f32[2,64,1536]{2,1,0:T(8,128)} %squeeze.14, f32[2,64,1536]{2,1,0:T(8,128)} %neg.3, f32[2,64,1536]{2,1,0:T(8,128)S(1)} %copy-done.1, f32[2,96,1536]{2,1,0:T(8,128)} %squeeze.17, f32[2,96,1536]{2,1,0:T(8,128)} %squeeze.16), kind=kOutput, calls=%fused_computation | convolution fusion | flops 908918784 | bytes 4816896 | tf_op jit(solution)/shard_map/tmk,tnk->tmn/dot_general | solution.py:24
  26.1 0.1 fusion.14
  26.1 0.1 copy.21
  26.2 0.1 stack.10
  26.4 0.1 copy.20
  26.5 0.1 stack.9
  26.6 0.0 copy-done.2
  26.6 0.0 copy-done.3
  26.6 0.1 compare_select_fusion.1
  26.7 0.1 broadcast_multiply_fusion
  26.8 0.1 broadcast_in_dim.30
  26.8 0.1 mul.51
  27.0 0.1 mul.53
  27.1 0.1 maximum_multiply_fusion
  27.2 15.8 %all_gather.3 = f32[8,2,2,6144]{3,2,1,0:T(2,128)S(1)} all-gather(f32[1,2,2,6144]{3,2,1,0:T(2,128)S(1)} %maximum_multiply_fusion), channel_id=1, replica_groups=mesh['ta'=4,'sa'=8] {'sa'}, dimensions={0}, use_global_device_ids=true | all-gather | bytes 884736 | tf_op jit(solution)/shard_map/all_gather | solution.py:44
  42.9 0.3 reduce_sum.18
  43.2 0.6 constant_dynamic-slice_fusion
  43.8 0.6 multiply_reduce_fusion
  44.4 40.3 %psum.7 = f32[3,8]{1,0:T(4,128)S(1)} all-reduce(f32[3,8]{1,0:T(4,128)S(1)} %multiply_reduce_fusion), channel_id=1, replica_groups=mesh['ta'=4,'sa'=8] {'ta','sa'}, use_global_device_ids=true, to_apply=%region_2.3 | all-reduce | flops 24 | bytes 192 | tf_op jit(solution)/shard_map/psum | solution.py:43
  84.7 0.6 broadcast_multiply_fusion.1
  (3 shorter events, 0.0 us)
Async XLA Ops:
  5.0 5.4 %copy-start = (f32[2,2,3,8,4,3,512]{6,4,5,3,2,1,0:T(4,128)S(1)}, f32[2,2,3,8,4,3,512]{6,4,5,3,2,1,0:T(4,128)}, u32[]{:S(2)}) copy-start(f32[2,2,3,8,4,3,512]{6,4,5,3,2,1,0:T(4,128)} %param.5) | copy-start | bytes 7077892
  17.4 2.9 %copy-start.1 = (f32[2,64,1536]{2,1,0:T(8,128)S(1)}, f32[2,64,1536]{2,1,0:T(8,128)}, u32[]{:S(2)}) copy-start(f32[2,64,1536]{2,1,0:T(8,128)} %squeeze.15) | copy-start | bytes 2359300
  20.3 6.2 %copy-start.2 = (s32[3,8]{1,0:T(4,128)S(1)}, s32[3,8]{1,0:T(4,128)}, u32[]{:S(2)}) copy-start(s32[3,8]{1,0:T(4,128)} %param.7) | copy-start | bytes 292
  20.3 6.3 %copy-start.3 = (s32[3]{0:T(128)S(1)}, s32[3]{0:T(128)}, u32[]{:S(2)}) copy-start(s32[3]{0:T(128)} %param.6) | copy-start | bytes 40
